TPU v7x, 32 devices: a whole 2x2x4 slice. The times are simulated.
32 devices in a mesh: tok: 4 (over y, x), din: 4 (over z), dout: 2 (over core).
Axes of the slice: x: 2, y: 2, z: 4, core: 2. Of those that a mesh axis runs over, the one named last changes fastest.
Arguments:
- inputs: bfloat16 [1024, 7168], P(('tok', 'dout'), 'din'), may hold values from -6 to 6
- out_grad: bfloat16 [1024, 9216], P(('tok', 'din'), 'dout'), may hold values from -0.1875 to 0.1875
Outputs:
- weight_grad: bfloat16 [7168, 9216], P(('din', 'tok'), 'dout')
All inputs are finite; a program needn't handle non-finite values.
Results may differ from a plain program's by a relative error of at most 0.014.
Values may be sent and summed in bfloat16 or wider, within the bound.
A program may use at most 64 MiB of HBM per device.

v0:
```python
import functools

import jax
import jax.numpy as jnp
from jax import lax
from jax.experimental import pallas as pl
from jax.experimental.pallas import tpu as pltpu
from jax.sharding import PartitionSpec as P

MESH = pl.DeviceIdType.MESH
LANES = 128
KINDS = 4


def scattered(inputs, out_grad):
    gathered = lax.all_gather(inputs, "dout", axis=0, tiled=True)
    partial_term = lax.dot_general(
        gathered,
        lax.all_gather(out_grad, "din", axis=0, tiled=True),
        (((0,), (0,)), ((), ())),
        preferred_element_type=jnp.float32,
    )
    return lax.psum_scatter(
        partial_term.astype(jnp.bfloat16), "tok", scatter_dimension=0, tiled=True
    )


def kernel(sizes, a_ref, g_ref, o_ref, held, windows, turned, left, made,
           load_sem, a_load, a_send, a_recv, a_pass, a_got, z_send, z_recv, p_send, p_recv, o_sem):
    depth, chunks, rows, window = sizes
    t, z, core = lax.axis_index("tok"), lax.axis_index("din"), lax.axis_index("dout")
    y, x = t // 2, t % 2
    tx, ty = y * 2 + (1 - x), (1 - y) * 2 + x
    td = (1 - y) * 2 + (1 - x)
    wide = KINDS * LANES

    def at_t(other):
        return (other, z, core)

    partner = (t, z, 1 - core)

    def own(c, k):
        return pltpu.make_async_copy(
            g_ref.at[:, pl.ds(pl.multiple_of(c * wide + k * LANES, LANES), LANES)],
            held.at[c, k, y, x, z],
            load_sem.at[c, k],
        )

    def load(c, carry):
        for k in range(KINDS):
            own(c, k).start()
        return carry

    lax.fori_loop(0, chunks, load, 0)

    barrier = pltpu.get_barrier_semaphore()
    for other in (at_t(tx), at_t(ty), at_t(td), partner):
        pl.semaphore_signal(barrier, inc=1, device_id=other, device_id_type=MESH)

    @pl.when(z > 0)
    def _():
        pl.semaphore_signal(barrier, inc=1, device_id=(t, z - 1, core), device_id_type=MESH)

    @pl.when(z < depth - 1)
    def _():
        pl.semaphore_signal(barrier, inc=1, device_id=(t, z + 1, core), device_id_type=MESH)

    pl.semaphore_wait(barrier, 4 + jnp.where(z > 0, 1, 0) + jnp.where(z < depth - 1, 1, 0))

    def slab(owner):
        start = pl.multiple_of((owner * rows) // LANES * LANES, LANES)
        return a_ref.at[:, pl.ds(start, window)]

    def a_copy(j, target):
        return pltpu.make_async_remote_copy(
            src_ref=slab(target), dst_ref=windows.at[t, core],
            send_sem=a_send.at[j], recv_sem=a_recv.at[j],
            device_id=at_t(target), device_id_type=MESH,
        )

    def a_wait(j, source):
        pltpu.make_async_remote_copy(
            src_ref=slab(source), dst_ref=windows.at[source, core],
            send_sem=a_send.at[j], recv_sem=a_recv.at[j],
            device_id=at_t(source), device_id_type=MESH,
        ).wait_recv()

    def a_over(j, source, src):
        return pltpu.make_async_remote_copy(
            src_ref=src, dst_ref=windows.at[source, core],
            send_sem=a_pass.at[j], recv_sem=a_got.at[j],
            device_id=partner, device_id_type=MESH,
        )

    def a_over_wait(j, source):
        pltpu.make_async_remote_copy(
            src_ref=windows.at[source, 1 - core], dst_ref=windows.at[source, 1 - core],
            send_sem=a_pass.at[j], recv_sem=a_got.at[j],
            device_id=partner, device_id_type=MESH,
        ).wait_recv()

    mine = pltpu.make_async_copy(slab(t), windows.at[t, core], a_load)
    mine.start()

    def by_form(c, act):
        plain = (c > 0) & (c % 3 == 0)

        @pl.when(plain)
        def _():
            act(True)

        @pl.when(jnp.logical_not(plain))
        def _():
            act(False)

    def order_of(k, plain):
        return k + 2 if plain and k < 2 else k

    def early(plain):
        return [k for k in range(KINDS) if order_of(k, plain) < 2]

    def late(plain):
        return [k for k in range(KINDS) if order_of(k, plain) >= 2]

    def plane_ref(c, k, order, last, yy, xx):
        if order == 0:
            return held.at[c, k, yy] if last else held.at[c, k, yy, xx]
        if order == 1:
            return held.at[c, k, :, xx] if last else held.at[c, k, yy, xx]
        if not last:
            return held.at[c, k, yy, xx, z]
        return held.at[c, k, yy] if order == 2 else held.at[c, k, :, xx]

    def along_x(order, last):
        return (order in (0, 2)) != last

    def plane_to(c, k, order, last, ref):
        return pltpu.make_async_remote_copy(
            src_ref=ref, dst_ref=ref,
            send_sem=p_send.at[c, k, int(last)], recv_sem=p_recv.at[c, k, int(last)],
            device_id=at_t(tx if along_x(order, last) else ty), device_id_type=MESH,
        )

    def plane(c, k, plain, last):
        order = order_of(k, plain)
        return plane_to(c, k, order, last, plane_ref(c, k, order, last, y, x))

    def plane_wait(c, k, plain, last):
        order = order_of(k, plain)
        yy, xx = (y, 1 - x) if along_x(order, last) else (1 - y, x)
        plane_to(c, k, order, last, plane_ref(c, k, order, last, yy, xx)).wait_recv()

    def groups(plain):
        return late(plain) + ([] if plain else [0])

    def line_ref(c, g, plain, source):
        order = order_of(g, plain)
        if order == 0:
            return held.at[c, pl.ds(0, 2), y, x, source]
        return held.at[c, g, y, :, source] if order == 2 else held.at[c, g, :, x, source]

    def line(c, g, plain, source, up):
        ref = line_ref(c, g, plain, source)
        return pltpu.make_async_remote_copy(
            src_ref=ref, dst_ref=ref,
            send_sem=z_send.at[c, g, source, up], recv_sem=z_recv.at[c, g, source],
            device_id=(t, z + 1 if up else z - 1, core), device_id_type=MESH,
        )

    def both_ways(c, g, plain):
        @pl.when(z < depth - 1)
        def _():
            line(c, g, plain, z, 1).start()

        @pl.when(z > 0)
        def _():
            line(c, g, plain, z, 0).start()

    def first(c, carry):
        for k in range(KINDS):
            own(c, k).wait()

        def act(plain):
            for k in late(plain):
                plane(c, k, plain, False).start()

        by_form(c, act)
        return carry

    def send_early(c):
        def act(plain):
            if not plain:
                both_ways(c, 0, plain)

        by_form(c, act)

    def send_late(c):
        def act(plain):
            for k in late(plain):
                plane_wait(c, k, plain, False)
                both_ways(c, k, plain)

        by_form(c, act)

    def pass_on(c, hop):
        def act(plain):
            for g in sorted(groups(plain)):
                @pl.when(z - hop >= 0)
                def _():
                    line(c, g, plain, z - hop, 0).wait_recv()

                    @pl.when(z < depth - 1)
                    def _():
                        line(c, g, plain, z - hop, 1).start()

                @pl.when(z + hop < depth)
                def _():
                    line(c, g, plain, z + hop, 1).wait_recv()

                    @pl.when(z > 0)
                    def _():
                        line(c, g, plain, z + hop, 0).start()

        by_form(c, act)

    def spread(c):
        def act(plain):
            for k in early(plain):
                plane(c, k, plain, False).start()
            for k in late(plain):
                plane(c, k, plain, True).start()

        by_form(c, act)

    def finish(c):
        def act(plain):
            for k in early(plain):
                plane_wait(c, k, plain, False)
                plane(c, k, plain, True).start()

        by_form(c, act)

    def arrived(c):
        def act(plain):
            for k in range(KINDS):
                plane_wait(c, k, plain, True)

        by_form(c, act)

    def out_copy(c):
        return pltpu.make_async_copy(
            made.at[c], o_ref.at[:, pl.ds(pl.multiple_of(c * wide, LANES), wide)], o_sem.at[c]
        )

    def multiply(c):
        arrived(c)
        for k in range(0, KINDS, 2):
            pair = [held[c, k + i].reshape(-1, LANES) for i in range(2)]
            term = jnp.dot(
                left[...], jnp.concatenate(pair, axis=1), preferred_element_type=jnp.float32
            )
            made[c, :, k * LANES:(k + 2) * LANES] = term.astype(made.dtype)
        out_copy(c).start()

    first(0, 0)
    send_early(0)
    lax.fori_loop(1, chunks, first, 0)
    for j, target in enumerate((tx, ty, td)):
        a_copy(j, target).start()
    a_over(3, t, slab(t)).start()
    send_late(0)
    for c in range(1, depth - 1):
        for back in range(c):
            pass_on(back, c - back)
        send_early(c)
        send_late(c)

    def share():
        for j, source in enumerate((tx, ty, td)):
            a_wait(j, source)
            a_over(j, source, windows.at[source, core]).start()

    def turn():
        mine.wait()
        for j, source in enumerate((tx, ty, td, t)):
            a_over_wait(j, source)
        shift = pl.multiple_of((t * rows) % LANES, 16)
        piece = windows.shape[2]
        for j in range(windows.shape[0] * 2):
            turned[...] = windows[j // 2, j % 2].T
            left[:, j * piece:(j + 1) * piece] = turned[pl.ds(shift, rows), :]

    def step(i, carry):
        @pl.when(i < chunks)
        def _():
            pass_on(i, depth - 1)
            spread(i)

        for hop in range(depth - 2, 0, -1):
            ahead = depth - 1 - hop

            @pl.when(i + ahead < chunks)
            def _():
                pass_on(i + ahead, hop)

        @pl.when(i + depth - 1 < chunks)
        def _():
            send_early(i + depth - 1)
            send_late(i + depth - 1)

        @pl.when(i == 0)
        def _():
            share()

        @pl.when(i == 1)
        def _():
            turn()

        @pl.when((i >= 1) & (i < chunks + 1))
        def _():
            finish(i - 1)

        @pl.when(i >= 2)
        def _():
            multiply(i - 2)

        return carry

    lax.fori_loop(0, chunks + 2, step, 0)

    for j, target in enumerate((tx, ty, td)):
        a_copy(j, target).wait_send()
        a_over(j, target, windows.at[target, core]).wait_send()
    a_over(3, t, slab(t)).wait_send()

    def drain(c, carry):
        def act(plain):
            for k in range(KINDS):
                for last in (False, True):
                    plane(c, k, plain, last).wait_send()
            for g in groups(plain):
                for source in range(depth):
                    @pl.when((z < depth - 1) & (z >= source))
                    def _():
                        line(c, g, plain, source, 1).wait_send()

                    @pl.when((z > 0) & (z <= source))
                    def _():
                        line(c, g, plain, source, 0).wait_send()

        by_form(c, act)
        out_copy(c).wait()
        return carry

    lax.fori_loop(0, chunks, drain, 0)


def gathered(shape, inputs, out_grad):
    depth = shape["din"]
    groups = shape["tok"]
    rows = inputs.shape[1] // groups
    window = max((j * rows) % LANES for j in range(groups)) + rows
    window = -(-window // LANES) * LANES
    piece = inputs.shape[0]
    tall, columns = out_grad.shape
    wide = KINDS * LANES
    chunks = columns // wide
    tokens = tall * depth * groups
    any_ref = pl.BlockSpec(memory_space=pl.ANY)
    dma = pltpu.SemaphoreType.DMA
    return pl.pallas_call(
        functools.partial(kernel, (depth, chunks, rows, window)),
        out_shape=jax.ShapeDtypeStruct((rows, columns), out_grad.dtype),
        in_specs=[pl.BlockSpec(memory_space=pltpu.HBM)] * 2,
        out_specs=any_ref,
        scratch_shapes=[
            pltpu.VMEM((chunks, KINDS, 2, 2, depth, tall, LANES), out_grad.dtype),
            pltpu.VMEM((groups, 2, piece, window), inputs.dtype),
            pltpu.VMEM((window, piece), inputs.dtype),
            pltpu.VMEM((rows, tokens), inputs.dtype),
            pltpu.VMEM((chunks, rows, wide), out_grad.dtype),
            dma((chunks, KINDS)),
            dma,
            dma((3,)),
            dma((3,)),
            dma((4,)),
            dma((4,)),
            dma((chunks, KINDS, depth, 2)),
            dma((chunks, KINDS, depth)),
            dma((chunks, KINDS, 2)),
            dma((chunks, KINDS, 2)),
            dma((chunks,)),
        ],
        compiler_params=pltpu.CompilerParams(
            collective_id=0, has_side_effects=True, vmem_limit_bytes=24 * 2**20
        ),
        cost_estimate=pl.CostEstimate(
            flops=2 * rows * tokens * columns,
            bytes_accessed=2 * rows * columns,
            transcendentals=0,
        ),
    )(inputs, out_grad)


def solution(mesh):
    shape = dict(mesh.shape)

    def local(inputs, out_grad):
        groups, depth = shape["tok"], shape["din"]
        rows = inputs.shape[1] // groups
        tall = out_grad.shape[0]
        spread = tall * (groups * depth - 1)
        summed = rows * (groups - 1) + tall * (depth - 1)
        fits = (
            groups == 4
            and shape["dout"] == 2
            and inputs.shape[0] == LANES
            and rows % 16 == 0
            and tall % 16 == 0
            and out_grad.shape[1] % (KINDS * LANES) == 0
        )
        if fits and spread < summed:
            return gathered(shape, inputs, out_grad)
        return scattered(inputs, out_grad)

    placed = (P(("tok", "dout"), "din"), P(("tok", "din"), "dout"))
    return jax.shard_map(
        local, mesh=mesh, in_specs=placed, out_specs=P(("din", "tok"), "dout"), check_vma=False
    )
```

profile of v0, /device:TPU:0, one launch (start us, length us, event | category | flops | bytes accessed | tf_op | source)
XLA Modules:
  0.0 94.7 jit_solution(14721599299373535264)
XLA Ops:
  0.0 0.0 copy-start
  0.0 1.1 %copy-done = bf16[64,4608]{1,0:T(8,128)(2,1)S(1)} copy-done((bf16[64,4608]{1,0:T(8,128)(2,1)S(1)}, bf16[64,4608]{1,0:T(8,128)(2,1)}, u32[]{:S(2)}) %copy-start) | copy-done | bytes 589848
  1.1 0.0 copy-start.1
  1.1 1.0 %copy-done.1 = bf16[128,1792]{1,0:T(8,128)(2,1)S(1)} copy-done((bf16[128,1792]{1,0:T(8,128)(2,1)S(1)}, bf16[128,1792]{1,0:T(8,128)(2,1)}, u32[]{:S(2)}) %copy-start.1) | copy-done | bytes 458776
  2.1 90.6 %shard_map.28 = bf16[448,4608]{1,0:T(8,128)(2,1)S(1)} custom-call(bf16[128,1792]{1,0:T(8,128)(2,1)S(1)} %copy-done.1, bf16[64,4608]{1,0:T(8,128)(2,1)S(1)} %copy-done), custom_call_target="tpu_custom_call" | custom-call | flops 4227858432 | bytes 4128768 | tf_op jit(solution)/shard_map/pallas_call | solution.py:371
  92.7 2.0 %copy.4 = bf16[448,4608]{1,0:T(8,128)(2,1)} copy(bf16[448,4608]{1,0:T(8,128)(2,1)S(1)} %shard_map.28) | data formatting | bytes 8257536
Async XLA Ops:
  0.0 1.1 %copy-start = (bf16[64,4608]{1,0:T(8,128)(2,1)S(1)}, bf16[64,4608]{1,0:T(8,128)(2,1)}, u32[]{:S(2)}) copy-start(bf16[64,4608]{1,0:T(8,128)(2,1)} %g_ref.1) | copy-start | bytes 1769476
  1.1 1.0 %copy-start.1 = (bf16[128,1792]{1,0:T(8,128)(2,1)S(1)}, bf16[128,1792]{1,0:T(8,128)(2,1)}, u32[]{:S(2)}) copy-start(bf16[128,1792]{1,0:T(8,128)(2,1)} %a_ref.1) | copy-start | bytes 1376260
where the time goes:
time: 94.9 us; the launch traced here: 94.7 us
  Pallas kernels  90.6 us (95%)
  local copies, waits for them, and re-layouts  4.07 us (4%)
    pallas_call x1, Pallas kernels, gathered(): pl.pallas_call(functools.partial(kernel, (depth, chunks, rows, window)),...  90.6 us
    unnamed x5, local copies, waits for them, and re-layouts  4.07 us

commit v1 on v0

v1 whole, which is shorter than its diff:
```python
import functools

import jax
import jax.numpy as jnp
from jax import lax
from jax.experimental import pallas as pl
from jax.experimental.pallas import tpu as pltpu
from jax.sharding import PartitionSpec as P

MESH = pl.DeviceIdType.MESH
LANES = 128
STRIPS = 2
WIDE = STRIPS * LANES


def scattered(inputs, out_grad):
    gathered = lax.all_gather(inputs, "dout", axis=0, tiled=True)
    partial_term = lax.dot_general(
        gathered,
        lax.all_gather(out_grad, "din", axis=0, tiled=True),
        (((0,), (0,)), ((), ())),
        preferred_element_type=jnp.float32,
    )
    return lax.psum_scatter(
        partial_term.astype(jnp.bfloat16), "tok", scatter_dimension=0, tiled=True
    )


def plan(columns):
    total = columns // WIDE
    whole = 2 - total % 2
    split = (total - whole) // 2
    places = [(split * (g + 1)) // whole + g if g < whole - 1 else split + g for g in range(whole)]
    return split, whole, places


def kernel(sizes, a_ref, g_ref, o_ref, give, held, full, away, windows, left, ship,
           give_load, own_load, full_load, a_load,
           swap_send, swap_recv, fx_send, fx_recv, fy_send, fy_recv,
           a_send, a_recv, p_send, p_recv,
           z_send, z_recv, y_send, y_recv, out_send, out_recv):
    depth, split, whole, places, rows = sizes
    units = split + whole
    t, z, core = lax.axis_index("tok"), lax.axis_index("din"), lax.axis_index("dout")
    y, x = t // 2, t % 2
    near_x = (y * 2 + (1 - x), z, core)
    near_y = ((1 - y) * 2 + x, z, core)
    partner = (t, z, 1 - core)
    half = split * WIDE
    pair = 2 * rows

    def columns_of(side, c):
        return pl.multiple_of(side * half + c * WIDE, WIDE)

    def strip(start, j):
        return g_ref.at[:, pl.ds(pl.multiple_of(start + j * LANES, LANES), LANES)]

    def give_in(c, j):
        return pltpu.make_async_copy(strip(columns_of(1 - x, c), j), give.at[c, j], give_load.at[c, j])

    def own_in(c, j):
        return pltpu.make_async_copy(strip(columns_of(x, c), j), held.at[c, y, x, z, j], own_load.at[c, j])

    def full_in(g, j):
        return pltpu.make_async_copy(
            strip(2 * half + g * WIDE, j), full.at[g, y, x, z, j], full_load.at[g, j]
        )

    def a_in(i):
        src = a_ref.at[:, pl.ds(pl.multiple_of((y if i == 0 else 1 - y) * pair, LANES), pair)]
        return pltpu.make_async_copy(src, windows.at[y, x, core] if i == 0 else away, a_load.at[i])

    def load(c, carry):
        for j in range(STRIPS):
            give_in(c, j).start()
            own_in(c, j).start()
        return carry

    load(0, 0)
    a_in(0).start()
    a_in(1).start()
    lax.fori_loop(1, split, load, 0)
    for g in range(whole):
        for j in range(STRIPS):
            full_in(g, j).start()

    barrier = pltpu.get_barrier_semaphore()
    for other in (near_x, near_y, partner):
        pl.semaphore_signal(barrier, inc=1, device_id=other, device_id_type=MESH)

    @pl.when(z > 0)
    def _():
        pl.semaphore_signal(barrier, inc=1, device_id=(t, z - 1, core), device_id_type=MESH)

    @pl.when(z < depth - 1)
    def _():
        pl.semaphore_signal(barrier, inc=1, device_id=(t, z + 1, core), device_id_type=MESH)

    pl.semaphore_wait(barrier, 3 + jnp.where(z > 0, 1, 0) + jnp.where(z < depth - 1, 1, 0))

    def remote(src, dst, send, recv, device):
        return pltpu.make_async_remote_copy(
            src_ref=src, dst_ref=dst, send_sem=send, recv_sem=recv,
            device_id=device, device_id_type=MESH,
        )

    def swap(c):
        return remote(give.at[c], held.at[c, y, x, z], swap_send.at[c], swap_recv.at[c], near_x)

    def swap_wait(c):
        ref = held.at[c, y, 1 - x, z]
        remote(ref, ref, swap_send.at[c], swap_recv.at[c], near_x).wait_recv()

    def full_x(g, side):
        ref = full.at[g, y, side, z]
        return remote(ref, ref, fx_send.at[g], fx_recv.at[g], near_x)

    def full_y(g, row):
        ref = full.at[g, row, :, z]
        return remote(ref, ref, fy_send.at[g], fy_recv.at[g], near_y)

    def a_out(i):
        src = (windows.at[y, x, core], away, windows.at[1 - y, x, core])[i]
        dst = (windows.at[y, x, core], windows.at[y, x, core], windows.at[1 - y, x, core])[i]
        return remote(src, dst, a_send.at[i], a_recv.at[i], near_y if i == 1 else near_x)

    def a_wait(i):
        ref = (windows.at[y, 1 - x, core], windows.at[1 - y, x, core], windows.at[1 - y, 1 - x, core])[i]
        remote(ref, ref, a_send.at[i], a_recv.at[i], near_y if i == 1 else near_x).wait_recv()

    def group(i):
        return ((y, 1 - x), (1 - y, x), (1 - y, 1 - x), (y, x))[i]

    def over(i, side):
        yy, xx = group(i)
        ref = windows.at[yy, xx, side]
        return remote(ref, ref, p_send.at[i], p_recv.at[i], partner)

    def line(u, ref, source, up):
        return remote(
            ref, ref, z_send.at[u, source, up], z_recv.at[u, source],
            (t, z + 1 if up else z - 1, core),
        )

    def to_y(u, c, source, row):
        ref = held.at[c, row, :, source]
        return remote(ref, ref, y_send.at[u, source], y_recv.at[u, source], near_y)

    def by_kind(u, on_split, on_whole):
        is_whole = functools.reduce(jnp.logical_or, [u == p for p in places])
        before = sum(jnp.where(u > p, 1, 0) for p in places)

        @pl.when(jnp.logical_not(is_whole))
        def _():
            on_split(u - before)

        @pl.when(is_whole)
        def _():
            on_whole(before)

    def both_ways(u, ref):
        @pl.when(z < depth - 1)
        def _():
            line(u, ref, z, 1).start()

        @pl.when(z > 0)
        def _():
            line(u, ref, z, 0).start()

    def start_own(u):
        def on_split(c):
            for j in range(STRIPS):
                own_in(c, j).wait()
            swap_wait(c)
            both_ways(u, held.at[c, y, :, z])
            to_y(u, c, z, y).start()

        def on_whole(g):
            full_y(g, 1 - y).wait_recv()
            both_ways(u, full.at[g, :, :, z])

        by_kind(u, on_split, on_whole)

    def pass_on(u, hop):
        def on(of, then):
            @pl.when(z - hop >= 0)
            def _():
                ref = of(z - hop)
                line(u, ref, z - hop, 0).wait_recv()

                @pl.when(z < depth - 1)
                def _():
                    line(u, ref, z - hop, 1).start()

                then(z - hop)

            @pl.when(z + hop < depth)
            def _():
                ref = of(z + hop)
                line(u, ref, z + hop, 1).wait_recv()

                @pl.when(z > 0)
                def _():
                    line(u, ref, z + hop, 0).start()

                then(z + hop)

        by_kind(
            u,
            lambda c: on(lambda s: held.at[c, y, :, s], lambda s: to_y(u, c, s, y).start()),
            lambda g: on(lambda s: full.at[g, :, :, s], lambda s: None),
        )

    def out(c, side):
        dst = o_ref.at[:, pl.ds(columns_of(side, c), WIDE)]
        return remote(ship.at[c], dst, out_send.at[c], out_recv.at[c], near_x)

    def term(side, block):
        wide = jnp.concatenate([block[:, :, :, j].reshape(-1, LANES) for j in range(STRIPS)], axis=1)
        return jnp.dot(left[side], wide, preferred_element_type=jnp.float32).astype(o_ref.dtype)

    def multiply(u):
        def on_split(c):
            for source in range(depth):
                to_y(u, c, source, 1 - y).wait_recv()
            ship[c] = term(1 - x, held.at[c])
            o_ref[:, pl.ds(columns_of(x, c), WIDE)] = term(x, held.at[c])
            out(c, x).start()

        def on_whole(g):
            o_ref[:, pl.ds(pl.multiple_of(2 * half + g * WIDE, WIDE), WIDE)] = term(x, full.at[g])

        by_kind(u, on_split, on_whole)

    def turn(i):
        yy, xx = group(i)
        for side in range(2):
            tall = windows[yy, xx, side].T
            at = pl.multiple_of(((yy * 2 + xx) * 2 + side) * LANES, LANES)
            for k in range(2):
                left[k, :, pl.ds(at, LANES)] = tall[k * rows:(k + 1) * rows]

    def send_swap(c, carry):
        for j in range(STRIPS):
            give_in(c, j).wait()
        swap(c).start()
        return carry

    first = min(split, max(places[0], 1))
    send_swap(0, 0)
    a_in(0).wait()
    a_in(1).wait()
    a_out(1).start()
    lax.fori_loop(1, min(2, first), send_swap, 0)
    a_out(0).start()
    over(3, core).start()
    lax.fori_loop(min(2, first), first, send_swap, 0)

    def step(s, carry):
        @pl.when(s < units)
        def _():
            start_own(s)

        for hop in range(depth - 1, 0, -1):
            @pl.when((s >= hop) & (s - hop < units))
            def _():
                pass_on(s - hop, hop)

        @pl.when(s == 1)
        def _():
            a_wait(1)
            a_out(2).start()
            over(1, core).start()
            for g in range(whole):
                for j in range(STRIPS):
                    full_in(g, j).wait()
                full_x(g, x).start()
            lax.fori_loop(first, split, send_swap, 0)

        @pl.when(s == 2)
        def _():
            a_wait(0)
            over(0, core).start()

        @pl.when(s == depth - 1)
        def _():
            for g in range(whole):
                full_x(g, 1 - x).wait_recv()
                full_y(g, y).start()
            for i in (3, 1, 0):
                over(i, 1 - core).wait_recv()
                turn(i)

        @pl.when(s == depth)
        def _():
            a_wait(2)
            over(2, core).start()
            over(2, 1 - core).wait_recv()
            turn(2)

        @pl.when(s >= depth)
        def _():
            multiply(s - depth)

        return carry

    lax.fori_loop(0, units + depth, step, 0)

    for i in range(3):
        a_out(i).wait_send()
    for i in range(4):
        over(i, core).wait_send()
    for g in range(whole):
        full_x(g, x).wait_send()
        full_y(g, y).wait_send()

    def drain(u, carry):
        def lines(ref_of):
            for source in range(depth):
                @pl.when((z < depth - 1) & (z >= source))
                def _():
                    line(u, ref_of(source), source, 1).wait_send()

                @pl.when((z > 0) & (z <= source))
                def _():
                    line(u, ref_of(source), source, 0).wait_send()

        def on_split(c):
            lines(lambda s: held.at[c, y, :, s])
            swap(c).wait_send()
            for source in range(depth):
                to_y(u, c, source, y).wait_send()
            out(c, x).wait_send()
            out(c, 1 - x).wait_recv()

        by_kind(u, on_split, lambda g: lines(lambda s: full.at[g, :, :, s]))
        return carry

    lax.fori_loop(0, units, drain, 0)


def gathered(shape, inputs, out_grad):
    depth = shape["din"]
    groups = shape["tok"]
    rows = inputs.shape[1] // groups
    piece = inputs.shape[0]
    tall, columns = out_grad.shape
    split, whole, places = plan(columns)
    units = split + whole
    tokens = tall * depth * groups
    kind = out_grad.dtype
    dma = pltpu.SemaphoreType.DMA
    return pl.pallas_call(
        functools.partial(kernel, (depth, split, whole, places, rows)),
        out_shape=jax.ShapeDtypeStruct((rows, columns), kind),
        in_specs=[pl.BlockSpec(memory_space=pltpu.HBM)] * 2,
        out_specs=pl.BlockSpec(memory_space=pltpu.VMEM),
        scratch_shapes=[
            pltpu.VMEM((split, STRIPS, tall, LANES), kind),
            pltpu.VMEM((split, 2, 2, depth, STRIPS, tall, LANES), kind),
            pltpu.VMEM((whole, 2, 2, depth, STRIPS, tall, LANES), kind),
            pltpu.VMEM((piece, 2 * rows), kind),
            pltpu.VMEM((2, 2, 2, piece, 2 * rows), kind),
            pltpu.VMEM((2, rows, tokens), kind),
            pltpu.VMEM((split, rows, WIDE), kind),
            dma((split, STRIPS)),
            dma((split, STRIPS)),
            dma((whole, STRIPS)),
            dma((2,)),
            dma((split,)),
            dma((split,)),
            dma((whole,)),
            dma((whole,)),
            dma((whole,)),
            dma((whole,)),
            dma((3,)),
            dma((3,)),
            dma((4,)),
            dma((4,)),
            dma((units, depth, 2)),
            dma((units, depth)),
            dma((units, depth)),
            dma((units, depth)),
            dma((split,)),
            dma((split,)),
        ],
        compiler_params=pltpu.CompilerParams(
            collective_id=0, has_side_effects=True, vmem_limit_bytes=59 * 2**20
        ),
        cost_estimate=pl.CostEstimate(
            flops=2 * rows * tokens * columns,
            bytes_accessed=2 * rows * columns,
            transcendentals=0,
        ),
    )(inputs, out_grad)


def solution(mesh):
    shape = dict(mesh.shape)

    def local(inputs, out_grad):
        groups, depth = shape["tok"], shape["din"]
        rows = inputs.shape[1] // groups
        tall, columns = out_grad.shape
        fits = (
            groups == 4
            and shape["dout"] == 2
            and 2 < depth <= 8
            and inputs.shape[0] == LANES
            and tall * depth == 2 * LANES
            and rows % 64 == 0
            and tall % 16 == 0
            and columns % WIDE == 0
            and columns >= 8 * WIDE
            and rows * columns <= 2**21
        )
        if fits:
            return gathered(shape, inputs, out_grad)
        return scattered(inputs, out_grad)

    placed = (P(("tok", "dout"), "din"), P(("tok", "din"), "dout"))
    return jax.shard_map(
        local, mesh=mesh, in_specs=placed, out_specs=P(("din", "tok"), "dout"), check_vma=False
    )
```

time: 94.9 us -> 87.1 us (0.918)
  Pallas kernels: 90.6 us -> 82.5 us
    pallas_call x1, Pallas kernels: 90.6 us -> 82.5 us  [gathered(): pl.pallas_call(functools.partial(kernel, (depth, split, whole, places, ro...]
    unnamed x5 -> x1, local copies, waits for them, and re-layouts: 4.07 us -> 4.42 us
where the time goes in v1:
time: 87.1 us; the launch traced here: 86.9 us
  Pallas kernels  82.5 us (95%)
  local copies, waits for them, and re-layouts  4.42 us (5%)
    pallas_call x1, Pallas kernels, gathered(): pl.pallas_call(functools.partial(kernel, (depth, split, whole, places, ro...  82.5 us
    unnamed x1, local copies, waits for them, and re-layouts  4.42 us

profile of v1, /device:TPU:0, one launch (start us, length us, event | category | flops | bytes accessed | tf_op | source)
XLA Modules:
  0.0 86.9 jit_solution(16860410183351584131)
XLA Ops:
  0.0 82.5 %shard_map.28 = bf16[448,4608]{1,0:T(8,128)(2,1)} custom-call(bf16[128,1792]{1,0:T(8,128)(2,1)} %a_ref.1, bf16[64,4608]{1,0:T(8,128)(2,1)} %g_ref.1), custom_call_target="tpu_custom_call" | custom-call | flops 4227858432 | bytes 4128768 | tf_op jit(solution)/shard_map/pallas_call | solution.py:353
  82.5 4.4 %copy.4 = bf16[448,4608]{1,0:T(8,128)(2,1)} copy(bf16[448,4608]{1,0:T(8,128)(2,1)} %shard_map.28) | data formatting | bytes 8257536

commit v2 on v1

--- a/solution.py
+++ b/solution.py
@@ -385,14 +385,14 @@
             dma((split,)),
         ],
         compiler_params=pltpu.CompilerParams(
-            collective_id=0, has_side_effects=True, vmem_limit_bytes=59 * 2**20
+            collective_id=0, has_side_effects=True, vmem_limit_bytes=40 * 2**20
         ),
         cost_estimate=pl.CostEstimate(
             flops=2 * rows * tokens * columns,
             bytes_accessed=2 * rows * columns,
             transcendentals=0,
         ),
-    )(inputs, out_grad)
+    )(*[pltpu.with_memory_space_constraint(v, pltpu.HBM) for v in (inputs, out_grad)])
 
 
 def solution(mesh):

time: 87.1 us -> 82.7 us (0.949)
  local copies, waits for them, and re-layouts: 4.42 us -> 1.99 us
  Pallas kernels: 82.5 us -> 80.6 us
    unnamed x1, local copies, waits for them, and re-layouts: 4.42 us -> 1.99 us
    pallas_call x1, Pallas kernels: 82.5 us -> 80.6 us  [gathered(): pl.pallas_call(functools.partial(kernel, (depth, split, whole, places, ro...]
where the time goes in v2:
time: 82.7 us; the launch traced here: 82.6 us
  Pallas kernels  80.6 us (97%)
  local copies, waits for them, and re-layouts  1.99 us (2%)
    pallas_call x1, Pallas kernels, gathered(): pl.pallas_call(functools.partial(kernel, (depth, split, whole, places, ro...  80.6 us
    unnamed x1, local copies, waits for them, and re-layouts  1.99 us

profile of v2, /device:TPU:0, one launch (start us, length us, event | category | flops | bytes accessed | tf_op | source)
XLA Modules:
  0.0 82.6 jit_solution(17276466983484170979)
XLA Ops:
  0.0 80.6 %shard_map.28 = bf16[448,4608]{1,0:T(8,128)(2,1)S(1)} custom-call(bf16[128,1792]{1,0:T(8,128)(2,1)} %a_ref.1, bf16[64,4608]{1,0:T(8,128)(2,1)} %g_ref.1), custom_call_target="tpu_custom_call" | custom-call | flops 4227858432 | bytes 4128768 | tf_op jit(solution)/shard_map/pallas_call | solution.py:353
  80.6 2.0 %copy.4 = bf16[448,4608]{1,0:T(8,128)(2,1)} copy(bf16[448,4608]{1,0:T(8,128)(2,1)S(1)} %shard_map.28) | data formatting | bytes 8257536

commit v3 on v2

v3 whole, which is shorter than its diff:
```python
import functools

import jax
import jax.numpy as jnp
from jax import lax
from jax.experimental import pallas as pl
from jax.experimental.pallas import tpu as pltpu
from jax.sharding import PartitionSpec as P

MESH = pl.DeviceIdType.MESH
LANES = 128
SPLIT, EARLY, WHOLE = range(3)
SWAP, A_NEAR_Y, A_NEAR_X, A_ON, A_TAKE, TURN_MOST, A_LAST, TURN_LAST, TO_Y, OWN, LINE, MULTIPLY = range(12)
UNITS = [(SPLIT, 1), (SPLIT, 2), (SPLIT, 2), (SPLIT, 2), (SPLIT, 2), (WHOLE, 2), (SPLIT, 2), (SPLIT, 2), (SPLIT, 2), (EARLY, 2)]
ORDER = [
    (0, 1), (1,), (0, 7), (0, 9), (0, 3), (2,), (9, 1), (0, 6), (9, 3),
    (10, 1, 3), (10, 1, 1), (10, 1, -3), (3,), (10, 3, 1), (4,), (0, 4), (10, 1, -1), (9, 7),
    (10, 1, 2), (5,), (0, 2), (10, 3, -3), (10, 1, -2), (0, 0), (0, 5), (8, 9), (10, 3, -1),
    (10, 3, 2), (9, 6), (6,), (10, 3, 3), (7,), (0, 8), (11, 1), (10, 3, -2), (10, 7, -1),
    (10, 7, 1), (9, 9), (10, 7, -3), (10, 7, 3), (10, 7, -2), (10, 6, -3), (10, 7, 2), (10, 6, 1), (11, 3),
    (10, 6, -1), (9, 8), (11, 7), (10, 6, 3), (10, 6, -2), (10, 6, 2), (10, 9, 3), (10, 9, 1), (10, 8, 1),
    (10, 8, -1), (10, 9, -1), (10, 8, 3), (11, 6), (10, 8, -3), (9, 2), (10, 8, -2), (10, 8, 2), (8, 5),
    (10, 9, -3), (10, 9, -2), (9, 0), (10, 9, 2), (11, 9), (10, 2, 1), (10, 2, -1), (11, 8), (9, 4),
    (10, 2, -3), (10, 2, 2), (10, 2, -2), (10, 2, 3), (10, 4, 3), (10, 0, 1), (10, 0, 3), (10, 0, -1), (10, 0, -3),
    (10, 0, -2), (10, 0, 2), (10, 4, 1), (10, 4, -1), (10, 4, -3), (9, 5), (11, 2), (10, 4, 2), (11, 0),
    (10, 4, -2), (11, 4), (10, 5, -1), (10, 5, 1), (10, 5, 3), (10, 5, -2), (10, 5, 2), (10, 5, -3), (11, 5),
]


def scattered(inputs, out_grad):
    gathered = lax.all_gather(inputs, "dout", axis=0, tiled=True)
    partial_term = lax.dot_general(
        gathered,
        lax.all_gather(out_grad, "din", axis=0, tiled=True),
        (((0,), (0,)), ((), ())),
        preferred_element_type=jnp.float32,
    )
    return lax.psum_scatter(
        partial_term.astype(jnp.bfloat16), "tok", scatter_dimension=0, tiled=True
    )


def plan(strips, depth):
    if depth == 4 and sum(n * (1 if form == WHOLE else 2) for form, n in UNITS) == strips:
        return UNITS, ORDER
    units = [(SPLIT, 2)] * (strips // 4) + [(WHOLE, 2)] * (strips % 4 // 2)
    return units, plain_order(units, depth)


def plain_order(units, depth):
    reach = depth - 1
    split = [u for u, (kind, _) in enumerate(units) if kind != WHOLE]
    acts = [(SWAP, split[0]), (A_NEAR_Y,)] + [(SWAP, u) for u in split[1:5]] + [(A_NEAR_X,)]
    acts += [(SWAP, u) for u in range(len(units)) if u not in split] + [(SWAP, u) for u in split[5:]]
    for s in range(len(units) + reach):
        if s < len(units):
            acts += [(TO_Y, s)] if units[s][0] != SPLIT else []
            acts.append((OWN, s))
        for hop in range(reach - 1, 0, -1):
            if 0 <= s - hop < len(units):
                acts += [(LINE, s - hop, -hop), (LINE, s - hop, hop)]
                if hop == reach - 1:
                    acts += [(LINE, s - hop, -reach), (LINE, s - hop, reach)]
        if s == 1:
            acts += [(A_ON,)]
        if s == 2:
            acts += [(A_TAKE,), (TURN_MOST,), (A_LAST,), (TURN_LAST,)]
        if s >= reach:
            acts.append((MULTIPLY, s - reach))
    return acts


def kernel(sizes, a_ref, g_ref, o_ref, *scratch):
    depth, rows, units, order = sizes
    count = len(units)
    scratch = list(scratch)
    held = [scratch.pop(0) for _ in units]
    give = [scratch.pop(0) if kind != WHOLE else None for kind, _ in units]
    ship = [scratch.pop(0) if kind != WHOLE else None for kind, _ in units]
    (away, windows, left, own_load, give_load, a_load, a_send, a_recv, p_send, p_recv,
     x_send, x_recv, y_send, y_recv, z_send, z_recv, out_send, out_recv) = scratch
    t, z, core = lax.axis_index("tok"), lax.axis_index("din"), lax.axis_index("dout")
    y, x = t // 2, t % 2
    near_x = (y * 2 + (1 - x), z, core)
    near_y = ((1 - y) * 2 + x, z, core)
    partner = (t, z, 1 - core)
    ends = ((z == 0, depth - 1), (z == depth - 1, 0))
    half = sum(n for kind, n in units if kind != WHOLE) * LANES
    pair = 2 * rows
    starts = []
    for u, (kind, _) in enumerate(units):
        alike = [n for k, n in units[:u] if (k == WHOLE) == (kind == WHOLE)]
        starts.append(sum(alike) * LANES + (2 * half if kind == WHOLE else 0))

    def columns_of(u, side):
        return starts[u] if units[u][0] == WHOLE else pl.multiple_of(side * half + starts[u], LANES)

    def strip(u, side, j):
        return g_ref.at[:, pl.ds(columns_of(u, side) + j * LANES, LANES)]

    def own_in(u, j):
        return pltpu.make_async_copy(strip(u, x, j), held[u].at[y, x, z, j], own_load.at[u, j])

    def give_in(u, j):
        return pltpu.make_async_copy(strip(u, 1 - x, j), give[u].at[j], give_load.at[u, j])

    def a_in(i):
        src = a_ref.at[:, pl.ds(pl.multiple_of((y if i == 0 else 1 - y) * pair, LANES), pair)]
        return pltpu.make_async_copy(src, windows.at[y, x, core] if i == 0 else away, a_load.at[i])

    def load(u):
        for j in range(units[u][1]):
            if units[u][0] != WHOLE:
                give_in(u, j).start()
            own_in(u, j).start()

    first = next(act[1] for act in order if act[0] == SWAP)
    load(first)
    for i in (1, 0):
        a_in(i).start()
    for u in range(count):
        if u != first:
            load(u)

    barrier = pltpu.get_barrier_semaphore()
    for other in (near_x, near_y, partner):
        pl.semaphore_signal(barrier, inc=1, device_id=other, device_id_type=MESH)
    greeted = 3
    for there, to in ((z > 0, z - 1), (z < depth - 1, z + 1)) + ends:
        greeted += jnp.where(there, 1, 0)

        @pl.when(there)
        def _():
            pl.semaphore_signal(barrier, inc=1, device_id=(t, to, core), device_id_type=MESH)

    pl.semaphore_wait(barrier, greeted)

    def remote(src, dst, send, recv, device):
        return pltpu.make_async_remote_copy(
            src_ref=src, dst_ref=dst, send_sem=send, recv_sem=recv,
            device_id=device, device_id_type=MESH,
        )

    def swap(u):
        dst = held[u].at[y, x, z]
        return remote(dst if give[u] is None else give[u], dst, x_send.at[u], x_recv.at[u], near_x)

    def swap_wait(u):
        for j in range(units[u][1]):
            own_in(u, j).wait()
        ref = held[u].at[y, 1 - x, z]
        remote(ref, ref, x_send.at[u], x_recv.at[u], near_x).wait_recv()

    def to_y(u, source, row):
        ref = held[u].at[row, :, source]
        return remote(ref, ref, y_send.at[u, source], y_recv.at[u, source], near_y)

    def a_out(i):
        src = (windows.at[y, x, core], away, windows.at[1 - y, x, core])[i]
        dst = (windows.at[y, x, core], windows.at[y, x, core], windows.at[1 - y, x, core])[i]
        return remote(src, dst, a_send.at[i], a_recv.at[i], near_y if i == 1 else near_x)

    def group(i):
        return ((y, 1 - x), (1 - y, x), (1 - y, 1 - x), (y, x))[i]

    def a_wait(i):
        ref = windows.at[group(i) + (core,)]
        remote(ref, ref, a_send.at[i], a_recv.at[i], near_y if i == 1 else near_x).wait_recv()

    def over(i, side):
        ref = windows.at[group(i) + (side,)]
        return remote(ref, ref, p_send.at[i], p_recv.at[i], partner)

    def turn(i):
        yy, xx = group(i)
        for side in range(2):
            tall = windows[yy, xx, side].T
            at = pl.multiple_of(((yy * 2 + xx) * 2 + side) * LANES, LANES)
            for k in range(2):
                left[k, :, pl.ds(at, LANES)] = tall[k * rows:(k + 1) * rows]

    def line_ref(u, source):
        return held[u].at[y, :, source] if units[u][0] == SPLIT else held[u].at[:, :, source]

    def line(u, source, way, to):
        ref = line_ref(u, source)
        return remote(ref, ref, z_send.at[u, source, way], z_recv.at[u, source], (t, to, core))

    def own_lines(u, act):
        for way, (there, to) in enumerate(((z > 0, z - 1), (z < depth - 1, z + 1)) + ends):
            @pl.when(there)
            def _():
                act(line(u, z, min(way, 2), to))

    def forward(u, off, act):
        if abs(off) + 2 < depth:
            @pl.when((z > 0) if off > 0 else (z < depth - 1))
            def _():
                act(line(u, z + off, int(off < 0), z - 1 if off > 0 else z + 1))

    def there(off):
        return (z + off >= 0) & (z + off < depth)

    def line_step(u, off):
        @pl.when(there(off))
        def _():
            line(u, z + off, 2, z).wait_recv()
            forward(u, off, lambda c: c.start())
            if units[u][0] == SPLIT:
                to_y(u, z + off, y).start()

    def own_step(u):
        if units[u][0] == SPLIT:
            swap_wait(u)
            own_lines(u, lambda c: c.start())
            to_y(u, z, y).start()
        else:
            to_y(u, z, 1 - y).wait_recv()
            own_lines(u, lambda c: c.start())

    def out(u, side):
        dst = o_ref.at[:, pl.ds(columns_of(u, side), units[u][1] * LANES)]
        return remote(ship[u], dst, out_send.at[u], out_recv.at[u], near_x)

    def term(u, side):
        block = [held[u][:, :, :, j].reshape(-1, LANES) for j in range(units[u][1])]
        wide = block[0] if len(block) == 1 else jnp.concatenate(block, axis=1)
        return jnp.dot(left[side], wide, preferred_element_type=jnp.float32).astype(o_ref.dtype)

    def multiply(u):
        kind, n = units[u]
        if kind == SPLIT:
            for source in range(depth):
                to_y(u, source, 1 - y).wait_recv()
        if kind != WHOLE:
            ship[u][...] = term(u, 1 - x)
        o_ref[:, pl.ds(columns_of(u, x), n * LANES)] = term(u, x)
        if kind != WHOLE:
            out(u, x).start()

    for act in order:
        what, rest = act[0], act[1:]
        if what == SWAP:
            u = rest[0]
            for j in range(units[u][1]):
                (own_in if give[u] is None else give_in)(u, j).wait()
            swap(u).start()
        elif what == A_NEAR_Y:
            a_in(1).wait()
            a_out(1).start()
        elif what == A_NEAR_X:
            a_in(0).wait()
            a_out(0).start()
            over(3, core).start()
        elif what == A_ON:
            a_wait(1)
            a_out(2).start()
            over(1, core).start()
        elif what == A_TAKE:
            a_wait(0)
            over(0, core).start()
        elif what == TURN_MOST:
            for i in (3, 1, 0):
                over(i, 1 - core).wait_recv()
                turn(i)
        elif what == A_LAST:
            a_wait(2)
            over(2, core).start()
        elif what == TURN_LAST:
            over(2, 1 - core).wait_recv()
            turn(2)
        elif what == TO_Y:
            u = rest[0]
            if give[u] is None:
                ref = held[u].at[y, 1 - x, z]
                remote(ref, ref, x_send.at[u], x_recv.at[u], near_x).wait_recv()
            else:
                swap_wait(u)
            to_y(u, z, y).start()
        elif what == OWN:
            own_step(*rest)
        elif what == LINE:
            line_step(*rest)
        elif what == MULTIPLY:
            multiply(*rest)

    for i in range(3):
        a_out(i).wait_send()
    for i in range(4):
        over(i, core).wait_send()
    for u, (kind, _) in enumerate(units):
        swap(u).wait_send()
        own_lines(u, lambda c: c.wait_send())
        to_y(u, z, y).wait_send()
        for off in range(1 - depth, depth):
            if off:
                @pl.when(there(off))
                def _():
                    forward(u, off, lambda c: c.wait_send())
                    if kind == SPLIT:
                        to_y(u, z + off, y).wait_send()
        if kind != WHOLE:
            out(u, x).wait_send()
            out(u, 1 - x).wait_recv()


def gathered(shape, inputs, out_grad):
    depth = shape["din"]
    groups = shape["tok"]
    rows = inputs.shape[1] // groups
    piece = inputs.shape[0]
    tall, columns = out_grad.shape
    units, order = plan(columns // LANES, depth)
    count = len(units)
    most = max(n for _, n in units)
    tokens = tall * depth * groups
    kind = out_grad.dtype
    dma = pltpu.SemaphoreType.DMA
    return pl.pallas_call(
        functools.partial(kernel, (depth, rows, units, order)),
        out_shape=jax.ShapeDtypeStruct((rows, columns), kind),
        in_specs=[pl.BlockSpec(memory_space=pltpu.HBM)] * 2,
        out_specs=pl.BlockSpec(memory_space=pltpu.VMEM),
        scratch_shapes=[
            *[pltpu.VMEM((2, 2, depth, n, tall, LANES), kind) for _, n in units],
            *[pltpu.VMEM((n, tall, LANES), kind) for form, n in units if form != WHOLE],
            *[pltpu.VMEM((rows, n * LANES), kind) for form, n in units if form != WHOLE],
            pltpu.VMEM((piece, 2 * rows), kind),
            pltpu.VMEM((2, 2, 2, piece, 2 * rows), kind),
            pltpu.VMEM((2, rows, tokens), kind),
            dma((count, most)),
            dma((count, most)),
            dma((2,)),
            dma((3,)),
            dma((3,)),
            dma((4,)),
            dma((4,)),
            dma((count,)),
            dma((count,)),
            dma((count, depth)),
            dma((count, depth)),
            dma((count, depth, 3)),
            dma((count, depth)),
            dma((count,)),
            dma((count,)),
        ],
        compiler_params=pltpu.CompilerParams(
            collective_id=0, has_side_effects=True, vmem_limit_bytes=40 * 2**20
        ),
        cost_estimate=pl.CostEstimate(
            flops=2 * rows * tokens * columns,
            bytes_accessed=2 * rows * columns,
            transcendentals=0,
        ),
    )(*[pltpu.with_memory_space_constraint(v, pltpu.HBM) for v in (inputs, out_grad)])


def solution(mesh):
    shape = dict(mesh.shape)

    def local(inputs, out_grad):
        groups, depth = shape["tok"], shape["din"]
        rows = inputs.shape[1] // groups
        tall, columns = out_grad.shape
        fits = (
            groups == 4
            and shape["dout"] == 2
            and 2 < depth <= 8
            and inputs.shape[0] == LANES
            and tall * depth == 2 * LANES
            and rows % 64 == 0
            and tall % 16 == 0
            and columns % (2 * LANES) == 0
            and columns >= 16 * LANES
            and rows * columns <= 2**21
        )
        if fits:
            return gathered(shape, inputs, out_grad)
        return scattered(inputs, out_grad)

    placed = (P(("tok", "dout"), "din"), P(("tok", "din"), "dout"))
    return jax.shard_map(
        local, mesh=mesh, in_specs=placed, out_specs=P(("din", "tok"), "dout"), check_vma=False
    )
```

time: 82.7 us -> 72.6 us (0.88)
  Pallas kernels: 80.6 us -> 70.4 us
    pallas_call x1, Pallas kernels: 80.6 us -> 70.4 us  [gathered(): pl.pallas_call(functools.partial(kernel, (depth, rows, units, order)), ou...]
where the time goes in v3:
time: 72.6 us; the launch traced here: 72.4 us
  Pallas kernels  70.4 us (97%)
  local copies, waits for them, and re-layouts  1.99 us (3%)
    pallas_call x1, Pallas kernels, gathered(): pl.pallas_call(functools.partial(kernel, (depth, rows, units, order)), ou...  70.4 us
    unnamed x1, local copies, waits for them, and re-layouts  1.99 us

profile of v3, /device:TPU:0, one launch (start us, length us, event | category | flops | bytes accessed | tf_op | source)
XLA Modules:
  0.0 72.4 jit_solution(10469302755509655134)
XLA Ops:
  0.0 70.4 %shard_map.28 = bf16[448,4608]{1,0:T(8,128)(2,1)S(1)} custom-call(bf16[128,1792]{1,0:T(8,128)(2,1)} %a_ref.1, bf16[64,4608]{1,0:T(8,128)(2,1)} %g_ref.1), custom_call_target="tpu_custom_call" | custom-call | flops 4227858432 | bytes 4128768 | tf_op jit(solution)/shard_map/pallas_call | solution.py:319
  70.4 2.0 %copy.4 = bf16[448,4608]{1,0:T(8,128)(2,1)} copy(bf16[448,4608]{1,0:T(8,128)(2,1)S(1)} %shard_map.28) | data formatting | bytes 8257536

commit v4 on v3

--- a/solution.py
+++ b/solution.py
@@ -9,21 +9,22 @@
 
 MESH = pl.DeviceIdType.MESH
 LANES = 128
-SPLIT, EARLY, WHOLE = range(3)
+SPLIT, SPLIT_EARLY, WHOLE, WHOLE_EARLY = range(4)
 SWAP, A_NEAR_Y, A_NEAR_X, A_ON, A_TAKE, TURN_MOST, A_LAST, TURN_LAST, TO_Y, OWN, LINE, MULTIPLY = range(12)
-UNITS = [(SPLIT, 1), (SPLIT, 2), (SPLIT, 2), (SPLIT, 2), (SPLIT, 2), (WHOLE, 2), (SPLIT, 2), (SPLIT, 2), (SPLIT, 2), (EARLY, 2)]
+UNITS = [(SPLIT, 1), (SPLIT, 1), (SPLIT, 2), (SPLIT, 2), (SPLIT, 2), (WHOLE, 2), (SPLIT, 2), (WHOLE_EARLY, 2), (SPLIT, 2), (SPLIT_EARLY, 2), (SPLIT, 2)]
 ORDER = [
-    (0, 1), (1,), (0, 7), (0, 9), (0, 3), (2,), (9, 1), (0, 6), (9, 3),
-    (10, 1, 3), (10, 1, 1), (10, 1, -3), (3,), (10, 3, 1), (4,), (0, 4), (10, 1, -1), (9, 7),
-    (10, 1, 2), (5,), (0, 2), (10, 3, -3), (10, 1, -2), (0, 0), (0, 5), (8, 9), (10, 3, -1),
-    (10, 3, 2), (9, 6), (6,), (10, 3, 3), (7,), (0, 8), (11, 1), (10, 3, -2), (10, 7, -1),
-    (10, 7, 1), (9, 9), (10, 7, -3), (10, 7, 3), (10, 7, -2), (10, 6, -3), (10, 7, 2), (10, 6, 1), (11, 3),
-    (10, 6, -1), (9, 8), (11, 7), (10, 6, 3), (10, 6, -2), (10, 6, 2), (10, 9, 3), (10, 9, 1), (10, 8, 1),
-    (10, 8, -1), (10, 9, -1), (10, 8, 3), (11, 6), (10, 8, -3), (9, 2), (10, 8, -2), (10, 8, 2), (8, 5),
-    (10, 9, -3), (10, 9, -2), (9, 0), (10, 9, 2), (11, 9), (10, 2, 1), (10, 2, -1), (11, 8), (9, 4),
-    (10, 2, -3), (10, 2, 2), (10, 2, -2), (10, 2, 3), (10, 4, 3), (10, 0, 1), (10, 0, 3), (10, 0, -1), (10, 0, -3),
-    (10, 0, -2), (10, 0, 2), (10, 4, 1), (10, 4, -1), (10, 4, -3), (9, 5), (11, 2), (10, 4, 2), (11, 0),
-    (10, 4, -2), (11, 4), (10, 5, -1), (10, 5, 1), (10, 5, 3), (10, 5, -2), (10, 5, 2), (10, 5, -3), (11, 5),
+    (0, 8), (0, 0), (0, 1), (0, 10), (1,), (0, 9), (2,), (9, 8), (9, 0),
+    (9, 1), (9, 10), (0, 4), (8, 9), (10, 8, 1), (3,), (0, 5), (10, 8, -1), (4,),
+    (10, 8, 3), (10, 8, -3), (0, 7), (0, 2), (10, 8, 2), (0, 3), (10, 8, -2), (10, 10, -1), (10, 10, 1),
+    (9, 4), (6,), (5,), (9, 9), (0, 6), (10, 10, 2), (10, 10, -2), (10, 10, 3), (10, 0, 1),
+    (7,), (11, 8), (10, 10, -3), (10, 1, -1), (10, 1, 1), (10, 1, -3), (10, 0, -1), (9, 6), (11, 10),
+    (10, 1, -2), (10, 1, 2), (10, 4, -1), (10, 1, 3), (10, 4, 3), (10, 0, -2), (10, 9, -1), (10, 0, -3), (10, 0, 3),
+    (10, 0, 2), (10, 4, 1), (10, 9, 1), (11, 1), (10, 4, 2), (10, 6, 1), (10, 4, -3), (10, 4, -2), (10, 9, -3),
+    (11, 0), (8, 7), (9, 2), (10, 9, 2), (10, 9, 3), (10, 6, -1), (10, 9, -2), (9, 3), (11, 9),
+    (10, 6, 3), (11, 4), (10, 6, 2), (10, 6, -3), (10, 2, -1), (10, 6, -2), (10, 2, 1), (9, 5), (10, 2, -3),
+    (10, 2, -2), (10, 3, -3), (10, 2, 3), (10, 2, 2), (10, 3, 1), (10, 3, -1), (11, 6), (9, 7), (10, 3, -2),
+    (10, 3, 3), (10, 5, -3), (10, 3, 2), (11, 2), (10, 5, -1), (11, 3), (10, 7, -1), (10, 5, 1), (10, 7, 1),
+    (10, 5, -2), (10, 7, -3), (10, 7, -2), (10, 7, 3), (10, 5, 3), (10, 5, 2), (10, 7, 2), (11, 7), (11, 5),
 ]
 
 
@@ -41,20 +42,28 @@
 
 
 def plan(strips, depth):
-    if depth == 4 and sum(n * (1 if form == WHOLE else 2) for form, n in UNITS) == strips:
+    if depth == 4 and sum(n * (1 if is_whole(form) else 2) for form, n in UNITS) == strips:
         return UNITS, ORDER
     units = [(SPLIT, 2)] * (strips // 4) + [(WHOLE, 2)] * (strips % 4 // 2)
     return units, plain_order(units, depth)
 
 
+def is_whole(form):
+    return form >= WHOLE
+
+
+def is_early(form):
+    return form % 2 == 1
+
+
 def plain_order(units, depth):
     reach = depth - 1
-    split = [u for u, (kind, _) in enumerate(units) if kind != WHOLE]
+    split = [u for u, (form, _) in enumerate(units) if not is_whole(form)]
     acts = [(SWAP, split[0]), (A_NEAR_Y,)] + [(SWAP, u) for u in split[1:5]] + [(A_NEAR_X,)]
     acts += [(SWAP, u) for u in range(len(units)) if u not in split] + [(SWAP, u) for u in split[5:]]
     for s in range(len(units) + reach):
         if s < len(units):
-            acts += [(TO_Y, s)] if units[s][0] != SPLIT else []
+            acts += [(TO_Y, s)] if is_early(units[s][0]) else []
             acts.append((OWN, s))
         for hop in range(reach - 1, 0, -1):
             if 0 <= s - hop < len(units):
@@ -75,8 +84,8 @@
     count = len(units)
     scratch = list(scratch)
     held = [scratch.pop(0) for _ in units]
-    give = [scratch.pop(0) if kind != WHOLE else None for kind, _ in units]
-    ship = [scratch.pop(0) if kind != WHOLE else None for kind, _ in units]
+    give = [None if is_whole(form) else scratch.pop(0) for form, _ in units]
+    ship = [None if is_whole(form) else scratch.pop(0) for form, _ in units]
     (away, windows, left, own_load, give_load, a_load, a_send, a_recv, p_send, p_recv,
      x_send, x_recv, y_send, y_recv, z_send, z_recv, out_send, out_recv) = scratch
     t, z, core = lax.axis_index("tok"), lax.axis_index("din"), lax.axis_index("dout")
@@ -85,15 +94,15 @@
     near_y = ((1 - y) * 2 + x, z, core)
     partner = (t, z, 1 - core)
     ends = ((z == 0, depth - 1), (z == depth - 1, 0))
-    half = sum(n for kind, n in units if kind != WHOLE) * LANES
+    half = sum(n for form, n in units if not is_whole(form)) * LANES
     pair = 2 * rows
     starts = []
-    for u, (kind, _) in enumerate(units):
-        alike = [n for k, n in units[:u] if (k == WHOLE) == (kind == WHOLE)]
-        starts.append(sum(alike) * LANES + (2 * half if kind == WHOLE else 0))
+    for u, (form, _) in enumerate(units):
+        alike = [n for other, n in units[:u] if is_whole(other) == is_whole(form)]
+        starts.append(sum(alike) * LANES + (2 * half if is_whole(form) else 0))
 
     def columns_of(u, side):
-        return starts[u] if units[u][0] == WHOLE else pl.multiple_of(side * half + starts[u], LANES)
+        return starts[u] if is_whole(units[u][0]) else pl.multiple_of(side * half + starts[u], LANES)
 
     def strip(u, side, j):
         return g_ref.at[:, pl.ds(columns_of(u, side) + j * LANES, LANES)]
@@ -110,7 +119,7 @@
 
     def load(u):
         for j in range(units[u][1]):
-            if units[u][0] != WHOLE:
+            if give[u] is not None:
                 give_in(u, j).start()
             own_in(u, j).start()
 
@@ -146,8 +155,9 @@
         return remote(dst if give[u] is None else give[u], dst, x_send.at[u], x_recv.at[u], near_x)
 
     def swap_wait(u):
-        for j in range(units[u][1]):
-            own_in(u, j).wait()
+        if give[u] is not None:
+            for j in range(units[u][1]):
+                own_in(u, j).wait()
         ref = held[u].at[y, 1 - x, z]
         remote(ref, ref, x_send.at[u], x_recv.at[u], near_x).wait_recv()
 
@@ -180,7 +190,7 @@
                 left[k, :, pl.ds(at, LANES)] = tall[k * rows:(k + 1) * rows]
 
     def line_ref(u, source):
-        return held[u].at[y, :, source] if units[u][0] == SPLIT else held[u].at[:, :, source]
+        return held[u].at[:, :, source] if is_early(units[u][0]) else held[u].at[y, :, source]
 
     def line(u, source, way, to):
         ref = line_ref(u, source)
@@ -206,17 +216,17 @@
         def _():
             line(u, z + off, 2, z).wait_recv()
             forward(u, off, lambda c: c.start())
-            if units[u][0] == SPLIT:
+            if not is_early(units[u][0]):
                 to_y(u, z + off, y).start()
 
     def own_step(u):
-        if units[u][0] == SPLIT:
+        if is_early(units[u][0]):
+            to_y(u, z, 1 - y).wait_recv()
+            own_lines(u, lambda c: c.start())
+        else:
             swap_wait(u)
             own_lines(u, lambda c: c.start())
             to_y(u, z, y).start()
-        else:
-            to_y(u, z, 1 - y).wait_recv()
-            own_lines(u, lambda c: c.start())
 
     def out(u, side):
         dst = o_ref.at[:, pl.ds(columns_of(u, side), units[u][1] * LANES)]
@@ -228,14 +238,14 @@
         return jnp.dot(left[side], wide, preferred_element_type=jnp.float32).astype(o_ref.dtype)
 
     def multiply(u):
-        kind, n = units[u]
-        if kind == SPLIT:
+        form, n = units[u]
+        if not is_early(form):
             for source in range(depth):
                 to_y(u, source, 1 - y).wait_recv()
-        if kind != WHOLE:
+        if not is_whole(form):
             ship[u][...] = term(u, 1 - x)
         o_ref[:, pl.ds(columns_of(u, x), n * LANES)] = term(u, x)
-        if kind != WHOLE:
+        if not is_whole(form):
             out(u, x).start()
 
     for act in order:
@@ -271,11 +281,7 @@
             turn(2)
         elif what == TO_Y:
             u = rest[0]
-            if give[u] is None:
-                ref = held[u].at[y, 1 - x, z]
-                remote(ref, ref, x_send.at[u], x_recv.at[u], near_x).wait_recv()
-            else:
-                swap_wait(u)
+            swap_wait(u)
             to_y(u, z, y).start()
         elif what == OWN:
             own_step(*rest)
@@ -288,7 +294,7 @@
         a_out(i).wait_send()
     for i in range(4):
         over(i, core).wait_send()
-    for u, (kind, _) in enumerate(units):
+    for u, (form, _) in enumerate(units):
         swap(u).wait_send()
         own_lines(u, lambda c: c.wait_send())
         to_y(u, z, y).wait_send()
@@ -297,9 +303,9 @@
                 @pl.when(there(off))
                 def _():
                     forward(u, off, lambda c: c.wait_send())
-                    if kind == SPLIT:
+                    if not is_early(form):
                         to_y(u, z + off, y).wait_send()
-        if kind != WHOLE:
+        if not is_whole(form):
             out(u, x).wait_send()
             out(u, 1 - x).wait_recv()
 
@@ -323,8 +329,8 @@
         out_specs=pl.BlockSpec(memory_space=pltpu.VMEM),
         scratch_shapes=[
             *[pltpu.VMEM((2, 2, depth, n, tall, LANES), kind) for _, n in units],
-            *[pltpu.VMEM((n, tall, LANES), kind) for form, n in units if form != WHOLE],
-            *[pltpu.VMEM((rows, n * LANES), kind) for form, n in units if form != WHOLE],
+            *[pltpu.VMEM((n, tall, LANES), kind) for form, n in units if not is_whole(form)],
+            *[pltpu.VMEM((rows, n * LANES), kind) for form, n in units if not is_whole(form)],
             pltpu.VMEM((piece, 2 * rows), kind),
             pltpu.VMEM((2, 2, 2, piece, 2 * rows), kind),
             pltpu.VMEM((2, rows, tokens), kind),

time: 72.6 us -> 70.9 us (0.977)
  Pallas kernels: 70.4 us -> 68.8 us
    pallas_call x1, Pallas kernels: 70.4 us -> 68.8 us  [gathered(): pl.pallas_call(functools.partial(kernel, (depth, rows, units, order)), ou...]
where the time goes in v4:
time: 70.9 us; the launch traced here: 70.8 us
  Pallas kernels  68.8 us (97%)
  local copies, waits for them, and re-layouts  1.99 us (3%)
    pallas_call x1, Pallas kernels, gathered(): pl.pallas_call(functools.partial(kernel, (depth, rows, units, order)), ou...  68.8 us
    unnamed x1, local copies, waits for them, and re-layouts  1.99 us

profile of v4, /device:TPU:0, one launch (start us, length us, event | category | flops | bytes accessed | tf_op | source)
XLA Modules:
  0.0 70.8 jit_solution(1462771896029053118)
XLA Ops:
  0.0 68.8 %shard_map.28 = bf16[448,4608]{1,0:T(8,128)(2,1)S(1)} custom-call(bf16[128,1792]{1,0:T(8,128)(2,1)} %a_ref.1, bf16[64,4608]{1,0:T(8,128)(2,1)} %g_ref.1), custom_call_target="tpu_custom_call" | custom-call | flops 4227858432 | bytes 4128768 | tf_op jit(solution)/shard_map/pallas_call | solution.py:325
  68.8 2.0 %copy.4 = bf16[448,4608]{1,0:T(8,128)(2,1)} copy(bf16[448,4608]{1,0:T(8,128)(2,1)S(1)} %shard_map.28) | data formatting | bytes 8257536

commit v5 on v4

--- a/solution.py
+++ b/solution.py
@@ -10,21 +10,22 @@
 MESH = pl.DeviceIdType.MESH
 LANES = 128
 SPLIT, SPLIT_EARLY, WHOLE, WHOLE_EARLY = range(4)
-SWAP, A_NEAR_Y, A_NEAR_X, A_ON, A_TAKE, TURN_MOST, A_LAST, TURN_LAST, TO_Y, OWN, LINE, MULTIPLY = range(12)
+SWAP, A_NEAR_Y, A_NEAR_X, A_ON, A_TAKE, TURN_MOST, A_LAST, TURN_LAST, TO_Y, OWN, LINE, MULTIPLY, A_OTHER_X = range(13)
 UNITS = [(SPLIT, 1), (SPLIT, 1), (SPLIT, 2), (SPLIT, 2), (SPLIT, 2), (WHOLE, 2), (SPLIT, 2), (WHOLE_EARLY, 2), (SPLIT, 2), (SPLIT_EARLY, 2), (SPLIT, 2)]
 ORDER = [
-    (0, 8), (0, 0), (0, 1), (0, 10), (1,), (0, 9), (2,), (9, 8), (9, 0),
-    (9, 1), (9, 10), (0, 4), (8, 9), (10, 8, 1), (3,), (0, 5), (10, 8, -1), (4,),
-    (10, 8, 3), (10, 8, -3), (0, 7), (0, 2), (10, 8, 2), (0, 3), (10, 8, -2), (10, 10, -1), (10, 10, 1),
-    (9, 4), (6,), (5,), (9, 9), (0, 6), (10, 10, 2), (10, 10, -2), (10, 10, 3), (10, 0, 1),
-    (7,), (11, 8), (10, 10, -3), (10, 1, -1), (10, 1, 1), (10, 1, -3), (10, 0, -1), (9, 6), (11, 10),
-    (10, 1, -2), (10, 1, 2), (10, 4, -1), (10, 1, 3), (10, 4, 3), (10, 0, -2), (10, 9, -1), (10, 0, -3), (10, 0, 3),
-    (10, 0, 2), (10, 4, 1), (10, 9, 1), (11, 1), (10, 4, 2), (10, 6, 1), (10, 4, -3), (10, 4, -2), (10, 9, -3),
-    (11, 0), (8, 7), (9, 2), (10, 9, 2), (10, 9, 3), (10, 6, -1), (10, 9, -2), (9, 3), (11, 9),
-    (10, 6, 3), (11, 4), (10, 6, 2), (10, 6, -3), (10, 2, -1), (10, 6, -2), (10, 2, 1), (9, 5), (10, 2, -3),
-    (10, 2, -2), (10, 3, -3), (10, 2, 3), (10, 2, 2), (10, 3, 1), (10, 3, -1), (11, 6), (9, 7), (10, 3, -2),
-    (10, 3, 3), (10, 5, -3), (10, 3, 2), (11, 2), (10, 5, -1), (11, 3), (10, 7, -1), (10, 5, 1), (10, 7, 1),
-    (10, 5, -2), (10, 7, -3), (10, 7, -2), (10, 7, 3), (10, 5, 3), (10, 5, 2), (10, 7, 2), (11, 7), (11, 5),
+    (1,), (0, 8), (0, 10), (0, 9), (0, 6), (2,), (12,), (9, 8), (9, 10),
+    (10, 8, -1), (0, 4), (10, 8, 1), (9, 6), (3,), (8, 9), (10, 8, -2), (10, 8, 3), (0, 0),
+    (10, 8, -3), (4,), (10, 8, 2), (10, 10, -1), (10, 10, 1), (5,), (9, 4), (0, 7), (0, 5),
+    (6,), (0, 1), (10, 10, 3), (0, 2), (10, 10, -3), (10, 10, 2), (10, 10, -2), (10, 6, 1), (0, 3),
+    (10, 6, -1), (9, 0), (10, 6, 3), (7,), (9, 9), (11, 8), (10, 6, -2), (10, 6, -3), (11, 10),
+    (10, 6, 2), (10, 0, 1), (10, 0, -1), (10, 0, 3), (10, 4, -1), (10, 4, 1), (10, 9, 1), (10, 0, -3), (10, 0, -2),
+    (10, 0, 2), (10, 9, -1), (10, 4, -3), (9, 2), (11, 6), (10, 4, -2), (10, 4, 2), (10, 4, 3), (8, 7),
+    (11, 0), (10, 9, 3), (9, 3), (11, 4), (10, 9, 2), (10, 2, 1), (10, 2, -3), (10, 2, -1), (10, 2, 3),
+    (10, 9, -3), (9, 1), (10, 3, 3), (10, 9, -2), (11, 9), (10, 3, -1), (10, 2, -2), (10, 2, 2), (10, 3, -3),
+    (10, 3, 1), (9, 5), (10, 1, -1), (10, 3, -2), (11, 2), (10, 3, 2), (10, 1, 1), (10, 1, -3), (10, 1, -2),
+    (9, 7), (10, 5, -1), (10, 5, 1), (10, 1, 3), (10, 5, 3), (10, 1, 2), (11, 3), (10, 7, 1), (10, 5, -3),
+    (10, 5, -2), (10, 5, 2), (10, 7, -1), (11, 1), (11, 5), (10, 7, -2), (10, 7, 2), (10, 7, 3), (10, 7, -3),
+    (11, 7),
 ]
 
 
@@ -59,7 +60,7 @@
 def plain_order(units, depth):
     reach = depth - 1
     split = [u for u, (form, _) in enumerate(units) if not is_whole(form)]
-    acts = [(SWAP, split[0]), (A_NEAR_Y,)] + [(SWAP, u) for u in split[1:5]] + [(A_NEAR_X,)]
+    acts = [(SWAP, split[0]), (A_NEAR_Y,)] + [(SWAP, u) for u in split[1:5]] + [(A_NEAR_X,), (A_OTHER_X,)]
     acts += [(SWAP, u) for u in range(len(units)) if u not in split] + [(SWAP, u) for u in split[5:]]
     for s in range(len(units) + reach):
         if s < len(units):
@@ -166,15 +167,16 @@
         return remote(ref, ref, y_send.at[u, source], y_recv.at[u, source], near_y)
 
     def a_out(i):
-        src = (windows.at[y, x, core], away, windows.at[1 - y, x, core])[i]
-        dst = (windows.at[y, x, core], windows.at[y, x, core], windows.at[1 - y, x, core])[i]
+        src = (windows.at[y, x, core], away, windows.at[1 - y, x, core], windows.at[y, x, 1 - core])[i]
+        dst = windows.at[y, x, core] if i == 1 else src
         return remote(src, dst, a_send.at[i], a_recv.at[i], near_y if i == 1 else near_x)
 
     def group(i):
-        return ((y, 1 - x), (1 - y, x), (1 - y, 1 - x), (y, x))[i]
+        return ((y, 1 - x), (1 - y, x), (1 - y, 1 - x), (y, x), (y, 1 - x))[i]
 
     def a_wait(i):
-        ref = windows.at[group(i) + (core,)]
+        yy, xx = group(i) if i < 3 else (y, 1 - x)
+        ref = windows.at[yy, xx, 1 - core if i == 3 else core]
         remote(ref, ref, a_send.at[i], a_recv.at[i], near_y if i == 1 else near_x).wait_recv()
 
     def over(i, side):
@@ -260,19 +262,42 @@
             a_out(1).start()
         elif what == A_NEAR_X:
             a_in(0).wait()
-            a_out(0).start()
             over(3, core).start()
+
+            @pl.when(core == 1)
+            def _():
+                a_out(0).start()
+        elif what == A_OTHER_X:
+            @pl.when(core == 1)
+            def _():
+                over(3, 0).wait_recv()
+                a_out(3).start()
         elif what == A_ON:
             a_wait(1)
             a_out(2).start()
             over(1, core).start()
         elif what == A_TAKE:
-            a_wait(0)
-            over(0, core).start()
+            @pl.when(core == 1)
+            def _():
+                a_wait(0)
+                over(0, 1).start()
+                a_wait(3)
+                over(4, 0).start()
         elif what == TURN_MOST:
-            for i in (3, 1, 0):
-                over(i, 1 - core).wait_recv()
-                turn(i)
+            @pl.when(core == 0)
+            def _():
+                over(3, 1).wait_recv()
+
+            turn(3)
+            over(1, 1 - core).wait_recv()
+            turn(1)
+
+            @pl.when(core == 0)
+            def _():
+                over(0, 1).wait_recv()
+                over(4, 0).wait_recv()
+
+            turn(0)
         elif what == A_LAST:
             a_wait(2)
             over(2, core).start()
@@ -290,10 +315,18 @@
         elif what == MULTIPLY:
             multiply(*rest)
 
-    for i in range(3):
+    for i in (1, 2):
         a_out(i).wait_send()
-    for i in range(4):
+    for i in (1, 2, 3):
         over(i, core).wait_send()
+
+    @pl.when(core == 1)
+    def _():
+        for i in (0, 3):
+            a_out(i).wait_send()
+        over(0, 1).wait_send()
+        over(4, 0).wait_send()
+
     for u, (form, _) in enumerate(units):
         swap(u).wait_send()
         own_lines(u, lambda c: c.wait_send())
@@ -337,10 +370,10 @@
             dma((count, most)),
             dma((count, most)),
             dma((2,)),
-            dma((3,)),
-            dma((3,)),
             dma((4,)),
             dma((4,)),
+            dma((5,)),
+            dma((5,)),
             dma((count,)),
             dma((count,)),
             dma((count, depth)),

time: 70.9 us -> 69.8 us (0.984)
  Pallas kernels: 68.8 us -> 67.7 us
    pallas_call x1, Pallas kernels: 68.8 us -> 67.7 us  [gathered(): pl.pallas_call(functools.partial(kernel, (depth, rows, units, order)), ou...]
where the time goes in v5:
time: 69.8 us; the launch traced here: 69.7 us
  Pallas kernels  67.7 us (97%)
  local copies, waits for them, and re-layouts  1.99 us (3%)
    pallas_call x1, Pallas kernels, gathered(): pl.pallas_call(functools.partial(kernel, (depth, rows, units, order)), ou...  67.7 us
    unnamed x1, local copies, waits for them, and re-layouts  1.99 us

profile of v5, /device:TPU:0, one launch (start us, length us, event | category | flops | bytes accessed | tf_op | source)
XLA Modules:
  0.0 69.7 jit_solution(15510396393960919003)
XLA Ops:
  0.0 67.7 %shard_map.28 = bf16[448,4608]{1,0:T(8,128)(2,1)S(1)} custom-call(bf16[128,1792]{1,0:T(8,128)(2,1)} %a_ref.1, bf16[64,4608]{1,0:T(8,128)(2,1)} %g_ref.1), custom_call_target="tpu_custom_call" | custom-call | flops 4227858432 | bytes 4128768 | tf_op jit(solution)/shard_map/pallas_call | solution.py:358
  67.7 2.0 %copy.4 = bf16[448,4608]{1,0:T(8,128)(2,1)} copy(bf16[448,4608]{1,0:T(8,128)(2,1)S(1)} %shard_map.28) | data formatting | bytes 8257536

commit v6 on v5

--- a/solution.py
+++ b/solution.py
@@ -14,14 +14,14 @@
 UNITS = [(SPLIT, 1), (SPLIT, 1), (SPLIT, 2), (SPLIT, 2), (SPLIT, 2), (WHOLE, 2), (SPLIT, 2), (WHOLE_EARLY, 2), (SPLIT, 2), (SPLIT_EARLY, 2), (SPLIT, 2)]
 ORDER = [
     (1,), (0, 8), (0, 10), (0, 9), (0, 6), (2,), (12,), (9, 8), (9, 10),
-    (10, 8, -1), (0, 4), (10, 8, 1), (9, 6), (3,), (8, 9), (10, 8, -2), (10, 8, 3), (0, 0),
+    (10, 8, 1), (10, 8, -1), (0, 4), (9, 6), (3,), (8, 9), (10, 8, -2), (10, 8, 3), (0, 0),
     (10, 8, -3), (4,), (10, 8, 2), (10, 10, -1), (10, 10, 1), (5,), (9, 4), (0, 7), (0, 5),
     (6,), (0, 1), (10, 10, 3), (0, 2), (10, 10, -3), (10, 10, 2), (10, 10, -2), (10, 6, 1), (0, 3),
     (10, 6, -1), (9, 0), (10, 6, 3), (7,), (9, 9), (11, 8), (10, 6, -2), (10, 6, -3), (11, 10),
     (10, 6, 2), (10, 0, 1), (10, 0, -1), (10, 0, 3), (10, 4, -1), (10, 4, 1), (10, 9, 1), (10, 0, -3), (10, 0, -2),
     (10, 0, 2), (10, 9, -1), (10, 4, -3), (9, 2), (11, 6), (10, 4, -2), (10, 4, 2), (10, 4, 3), (8, 7),
     (11, 0), (10, 9, 3), (9, 3), (11, 4), (10, 9, 2), (10, 2, 1), (10, 2, -3), (10, 2, -1), (10, 2, 3),
-    (10, 9, -3), (9, 1), (10, 3, 3), (10, 9, -2), (11, 9), (10, 3, -1), (10, 2, -2), (10, 2, 2), (10, 3, -3),
+    (10, 9, -3), (9, 1), (10, 3, 3), (10, 9, -2), (11, 9), (10, 3, -1), (10, 2, 2), (10, 2, -2), (10, 3, -3),
     (10, 3, 1), (9, 5), (10, 1, -1), (10, 3, -2), (11, 2), (10, 3, 2), (10, 1, 1), (10, 1, -3), (10, 1, -2),
     (9, 7), (10, 5, -1), (10, 5, 1), (10, 1, 3), (10, 5, 3), (10, 1, 2), (11, 3), (10, 7, 1), (10, 5, -3),
     (10, 5, -2), (10, 5, 2), (10, 7, -1), (11, 1), (11, 5), (10, 7, -2), (10, 7, 2), (10, 7, 3), (10, 7, -3),

time: 69.8 us -> 69.8 us (level)
  no operation moved by 1% of the time
where the time goes in v6:
time: 69.8 us; the launch traced here: 69.7 us
  Pallas kernels  67.7 us (97%)
  local copies, waits for them, and re-layouts  1.99 us (3%)
    pallas_call x1, Pallas kernels, gathered(): pl.pallas_call(functools.partial(kernel, (depth, rows, units, order)), ou...  67.7 us
    unnamed x1, local copies, waits for them, and re-layouts  1.99 us

profile of v6, /device:TPU:0, one launch (start us, length us, event | category | flops | bytes accessed | tf_op | source)
XLA Modules:
  0.0 69.7 jit_solution(17495175729413288496)
XLA Ops:
  0.0 67.7 %shard_map.28 = bf16[448,4608]{1,0:T(8,128)(2,1)S(1)} custom-call(bf16[128,1792]{1,0:T(8,128)(2,1)} %a_ref.1, bf16[64,4608]{1,0:T(8,128)(2,1)} %g_ref.1), custom_call_target="tpu_custom_call" | custom-call | flops 4227858432 | bytes 4128768 | tf_op jit(solution)/shard_map/pallas_call | solution.py:358
  67.7 2.0 %copy.4 = bf16[448,4608]{1,0:T(8,128)(2,1)} copy(bf16[448,4608]{1,0:T(8,128)(2,1)S(1)} %shard_map.28) | data formatting | bytes 8257536

commit v7 on v6

--- a/solution.py
+++ b/solution.py
@@ -343,6 +343,18 @@
             out(u, 1 - x).wait_recv()
 
 
+def put_out(pieces, src, dst, sems):
+    rows = src.shape[0] // pieces
+    copies = [
+        pltpu.make_async_copy(src.at[pl.ds(i * rows, rows)], dst.at[pl.ds(i * rows, rows)], sems.at[i])
+        for i in range(pieces)
+    ]
+    for copy in copies:
+        copy.start()
+    for copy in copies:
+        copy.wait()
+
+
 def gathered(shape, inputs, out_grad):
     depth = shape["din"]
     groups = shape["tok"]
@@ -355,7 +367,7 @@
     tokens = tall * depth * groups
     kind = out_grad.dtype
     dma = pltpu.SemaphoreType.DMA
-    return pl.pallas_call(
+    made = pl.pallas_call(
         functools.partial(kernel, (depth, rows, units, order)),
         out_shape=jax.ShapeDtypeStruct((rows, columns), kind),
         in_specs=[pl.BlockSpec(memory_space=pltpu.HBM)] * 2,
@@ -392,6 +404,15 @@
             transcendentals=0,
         ),
     )(*[pltpu.with_memory_space_constraint(v, pltpu.HBM) for v in (inputs, out_grad)])
+    pieces = rows // 64
+    return pl.pallas_call(
+        functools.partial(put_out, pieces),
+        out_shape=jax.ShapeDtypeStruct((rows, columns), kind),
+        in_specs=[pl.BlockSpec(memory_space=pltpu.VMEM)],
+        out_specs=pl.BlockSpec(memory_space=pltpu.HBM),
+        scratch_shapes=[dma((pieces,))],
+        compiler_params=pltpu.CompilerParams(vmem_limit_bytes=2**20),
+    )(made)
 
 
 def solution(mesh):

time: 69.8 us -> 69.9 us (level)
  Pallas kernels: 67.7 us -> 69.7 us
  local copies, waits for them, and re-layouts: 1.99 us -> 0 us
    pallas_call x0 -> x1, Pallas kernels: none -> 2.04 us  [gathered(): pl.pallas_call(functools.partial(put_out, pieces), out_shape=jax.ShapeDty...]
    unnamed x1 -> x0, local copies, waits for them, and re-layouts: 1.99 us -> none
where the time goes in v7:
time: 69.9 us; the launch traced here: 69.8 us
  Pallas kernels  69.7 us (100%)
    pallas_call x1, Pallas kernels, gathered(): pl.pallas_call(functools.partial(kernel, (depth, rows, units, order)), ou...  67.7 us
    pallas_call x1, Pallas kernels, gathered(): pl.pallas_call(functools.partial(put_out, pieces), out_shape=jax.ShapeDty...  2.04 us

profile of v7, /device:TPU:0, one launch (start us, length us, event | category | flops | bytes accessed | tf_op | source)
XLA Modules:
  0.0 69.8 jit_solution(12059735623361238139)
XLA Ops:
  0.0 67.7 %shard_map.28.src = bf16[448,4608]{1,0:T(8,128)(2,1)S(1)} custom-call(bf16[128,1792]{1,0:T(8,128)(2,1)} %a_ref.1, bf16[64,4608]{1,0:T(8,128)(2,1)} %g_ref.1), custom_call_target="tpu_custom_call" | custom-call | flops 4227858432 | bytes 4128768 | tf_op jit(solution)/shard_map/pallas_call | solution.py:370
  67.7 2.0 %shard_map.29 = bf16[448,4608]{1,0:T(8,128)(2,1)} custom-call(bf16[448,4608]{1,0:T(8,128)(2,1)S(1)} %shard_map.28.src), custom_call_target="tpu_custom_call" | custom-call | tf_op jit(solution)/shard_map/pallas_call | solution.py:408
